TPU v7x, 32 devices: a whole 2x2x4 slice. The times are simulated.
32 devices in a mesh: zero: 8 (over y, x, core), width: 4 (over z).
Axes of the slice: x: 2, y: 2, z: 4, core: 2. Of those that a mesh axis runs over, the one named last changes fastest.
Arguments:
- train_query: bfloat16 [3584, 4096], P('zero', 'width'), may hold values from -0.09375 to 0.09375
- low_query: bfloat16 [3584, 32], P('zero'), may hold values from -0.09375 to 0.09375
- high_query: bfloat16 [32, 4096], P(None, 'width'), may hold values from -1 to 1
- train_key: bfloat16 [3584, 2048], P('zero', 'width'), may hold values from -0.09375 to 0.09375
- low_key: bfloat16 [3584, 32], P('zero'), may hold values from -0.09375 to 0.09375
- high_key: bfloat16 [32, 2048], P(None, 'width'), may hold values from -1 to 1
- train_value: bfloat16 [3584, 2048], P('zero', 'width'), may hold values from -0.09375 to 0.09375
- low_value: bfloat16 [3584, 32], P('zero'), may hold values from -0.09375 to 0.09375
- high_value: bfloat16 [32, 2048], P(None, 'width'), may hold values from -1 to 1
- train_mixed: bfloat16 [4096, 3584], P('width', 'zero'), may hold values from -0.09375 to 0.09375
- low_mixed: bfloat16 [4096, 32], P('width'), may hold values from -0.09375 to 0.09375
- high_mixed: bfloat16 [32, 3584], P(None, 'zero'), may hold values from -1 to 1
- norm_train: float32 [3584], P(('zero', 'width')), may hold values from 0.25 to 1.75
- norm_step: float32 [3584], P(('zero', 'width')), may hold values from -0.3 to 0.3
Outputs:
- ready_query: bfloat16 [4096, 3584], P('width')
- ready_key: bfloat16 [2048, 3584], P('width')
- ready_value: bfloat16 [2048, 3584], P('width')
- ready_mixed: bfloat16 [3584, 4096], P(None, 'width')
- serve_norm: bfloat16 [3584], replicated
All inputs are finite; a program needn't handle non-finite values.
Results may differ from a plain program's by a relative error of at most 0.001.
Values may be sent and summed in bfloat16 or wider, within the bound.
A program may use at most 128 MiB of HBM per device.

v0:
```python
import jax
import jax.numpy as jnp
from jax import lax
from jax.sharding import PartitionSpec as P

mix_rate = 0.5


def body(
    train_query,
    low_query,
    high_query,
    train_key,
    low_key,
    high_key,
    train_value,
    low_value,
    high_value,
    train_mixed,
    low_mixed,
    high_mixed,
    norm_train,
    norm_step,
):
    latest_query = train_query.astype(jnp.float32) + mix_rate * jnp.dot(
        low_query, high_query, preferred_element_type=jnp.float32
    )
    latest_key = train_key.astype(jnp.float32) + mix_rate * jnp.dot(
        low_key, high_key, preferred_element_type=jnp.float32
    )
    latest_value = train_value.astype(jnp.float32) + mix_rate * jnp.dot(
        low_value, high_value, preferred_element_type=jnp.float32
    )
    latest_mixed = train_mixed.astype(jnp.float32) + mix_rate * jnp.dot(
        low_mixed, high_mixed, preferred_element_type=jnp.float32
    )
    narrow_query, narrow_key, narrow_value, narrow_mixed = (
        latest_query.astype(jnp.bfloat16),
        latest_key.astype(jnp.bfloat16),
        latest_value.astype(jnp.bfloat16),
        latest_mixed.astype(jnp.bfloat16),
    )
    ready_query, ready_key, ready_value, ready_mixed = (
        lax.all_gather(narrow_query, "zero", axis=0, tiled=True),
        lax.all_gather(narrow_key, "zero", axis=0, tiled=True),
        lax.all_gather(narrow_value, "zero", axis=0, tiled=True),
        lax.all_gather(narrow_mixed, "zero", axis=1, tiled=True),
    )
    ready_query, ready_key, ready_value, ready_mixed = (
        ready_query.T,
        ready_key.T,
        ready_value.T,
        ready_mixed.T,
    )
    serve_norm = lax.all_gather(
        (norm_train + norm_step).astype(jnp.bfloat16), ("zero", "width"), axis=0, tiled=True
    )
    return (ready_query, ready_key, ready_value, ready_mixed, serve_norm)


def solution(mesh):
    placed = (
        P("zero", "width"),
        P("zero", None),
        P(None, "width"),
        P("zero", "width"),
        P("zero", None),
        P(None, "width"),
        P("zero", "width"),
        P("zero", None),
        P(None, "width"),
        P("width", "zero"),
        P("width", None),
        P(None, "zero"),
        P(("zero", "width")),
        P(("zero", "width")),
    )
    return jax.shard_map(
        body,
        mesh=mesh,
        in_specs=placed,
        out_specs=(P("width", None), P("width", None), P("width", None), P(None, "width"), P()),
        check_vma=False,
    )
```

profile of v0, /device:TPU:0, one launch (start us, length us, event | category | flops | bytes accessed | tf_op | source)
XLA Modules:
  0.0 202.3 jit_solution(11500091203739998408)
XLA Ops:
  7.2 0.0 copy-start
  7.2 0.0 copy-start.1
  7.2 0.0 copy-start.4
  7.2 0.0 all-gather.7.cloned.1.call-start
  7.2 2.2 %fusion.2 = bf16[448,512]{1,0:T(8,128)(2,1)} fusion(bf16[448,32]{0,1:T(8,128)(2,1)} %param.18, bf16[32,512]{1,0:T(8,128)(2,1)} %param.19, bf16[448,512]{1,0:T(8,128)(2,1)} %param.17), kind=kOutput, calls=%fused_computation.6 | convolution fusion | flops 15597568 | bytes 978944 | tf_op jit(solution)/shard_map/dot_general | solution.py:28
  9.5 0.0 all-gather.7.cloned.1.call-update
  9.5 0.0 all-gather.9.cloned.1.call-start
  9.5 2.1 %fusion.3 = bf16[448,512]{1,0:T(8,128)(2,1)} fusion(bf16[448,32]{0,1:T(8,128)(2,1)} %param.21, bf16[32,512]{1,0:T(8,128)(2,1)} %param.22, bf16[448,512]{1,0:T(8,128)(2,1)} %param.20), kind=kOutput, calls=%fused_computation.7 | convolution fusion | flops 15597568 | bytes 978944 | tf_op jit(solution)/shard_map/dot_general | solution.py:31
  11.7 0.0 copy-start.2
  11.7 0.0 copy-start.3
  11.7 0.0 copy-start.5
  11.7 0.0 all-gather.9.cloned.1.call-update
  11.7 0.0 all-gather.5.cloned.1.call-start
  11.7 0.0 copy-done
  11.8 0.0 copy-done.1
  11.8 0.0 copy-done.4
  11.8 1.3 add_convert_fusion.1
  13.1 0.0 copy-start.6
  13.1 0.0 copy-start.7
  13.1 0.0 all-gather.5.cloned.1.call-update
  13.1 0.0 all-gather.11.cloned.1.call-start
  13.2 0.0 copy-done.2
  13.2 0.0 copy-done.3
  13.2 0.0 copy-done.5
  13.2 1.4 add_convert_fusion
  14.6 0.0 all-gather.11.cloned.1.call-update
  14.6 0.0 copy-done.6
  14.7 0.0 copy-done.7
  14.7 0.2 dynamic-update-slice
  14.9 42.3 %all-reduce = bf16[3584]{0:T(1024)(128)(2,1)} all-reduce(bf16[3584]{0:T(1024)(128)(2,1)S(1)} %dynamic-update-slice), channel_id=1, replica_groups=mesh['zero'=8,'width'=4] {'zero','width'}, use_global_device_ids=true, to_apply=%add | all-reduce | flops 3584 | bytes 14336
  57.2 0.0 all-gather.7.cloned.1.call-done
  57.2 6.0 %copy.20 = bf16[512,3584]{1,0:T(8,128)(2,1)} copy(bf16[512,3584]{0,1:T(8,128)(2,1)} %bitcast.14) | data formatting | bytes 7340032
  63.2 21.6 %all-gather.9.cloned.1.call-done = bf16[3584,512]{1,0:T(8,128)(2,1)} async-done(((bf16[448,512]{1,0:T(8,128)(2,1)}), bf16[3584,512]{1,0:T(8,128)(2,1)}) %all-gather.9.cloned.1.call-update) | async-done | bytes 3670032 | tf_op jit(solution)/shard_map/all_gather | solution.py:46
  84.8 5.9 %copy.21 = bf16[512,3584]{1,0:T(8,128)(2,1)} copy(bf16[512,3584]{0,1:T(8,128)(2,1)} %bitcast.15) | data formatting | bytes 7340032
  90.7 46.4 %all-gather.5.cloned.1.call-done = bf16[3584,1024]{1,0:T(8,128)(2,1)} async-done(((bf16[448,1024]{1,0:T(8,128)(2,1)}), bf16[3584,1024]{1,0:T(8,128)(2,1)}) %all-gather.5.cloned.1.call-update) | async-done | bytes 7340048 | tf_op jit(solution)/shard_map/all_gather | solution.py:44
  137.2 10.0 %copy.19 = bf16[1024,3584]{1,0:T(8,128)(2,1)} copy(bf16[1024,3584]{0,1:T(8,128)(2,1)} %bitcast.12) | data formatting | bytes 14680064
  147.2 41.6 %all-gather.11.cloned.1.call-done = bf16[1024,3584]{0,1:T(8,128)(2,1)} async-done(((bf16[1024,448]{0,1:T(8,128)(2,1)}), bf16[1024,3584]{0,1:T(8,128)(2,1)}) %all-gather.11.cloned.1.call-update) | async-done | bytes 7340048 | tf_op jit(solution)/shard_map/all_gather | solution.py:47
  188.8 7.0 %copy.24 = bf16[3584,1024]{1,0:T(8,128)(2,1)} copy(bf16[3584,1024]{1,0:T(8,128)(2,1)} %bitcast.13) | data formatting | bytes 14680064
  (2 shorter events, 0.0 us)
Async XLA Ops:
  7.2 4.6 %copy-start = (bf16[32,1024]{1,0:T(8,128)(2,1)S(1)}, bf16[32,1024]{1,0:T(8,128)(2,1)}, u32[]{:S(2)}) copy-start(bf16[32,1024]{1,0:T(8,128)(2,1)} %param.16) | copy-start | bytes 196612
  7.2 4.6 %copy-start.1 = (bf16[448,1024]{1,0:T(8,128)(2,1)S(1)}, bf16[448,1024]{1,0:T(8,128)(2,1)}, u32[]{:S(2)}) copy-start(bf16[448,1024]{1,0:T(8,128)(2,1)} %param.14) | copy-start | bytes 2752516
  7.2 4.6 %copy-start.4 = (bf16[448,32]{0,1:T(8,128)(2,1)S(1)}, bf16[448,32]{0,1:T(8,128)(2,1)}, u32[]{:S(2)}) copy-start(bf16[448,32]{0,1:T(8,128)(2,1)} %param.15) | copy-start | bytes 86020
  7.2 50.0 %all-gather.7.cloned.1.call-start = ((), (), s32[]{:S(2)}) async-start(), calls=%async_computation.1 | async-start | bytes 4128768 | tf_op jit(solution)/shard_map/all_gather | solution.py:45
  9.5 75.4 %all-gather.9.cloned.1.call-start = ((), (), s32[]{:S(2)}) async-start(), calls=%async_computation.2 | async-start | bytes 4128768 | tf_op jit(solution)/shard_map/all_gather | solution.py:46
  11.7 1.5 copy-start.2
  11.7 1.5 copy-start.3
  11.7 1.5 copy-start.5
  11.7 125.5 %all-gather.5.cloned.1.call-start = ((), (), s32[]{:S(2)}) async-start(), calls=%async_computation | async-start | bytes 8257536 | tf_op jit(solution)/shard_map/all_gather | solution.py:44
  13.1 1.5 copy-start.6
  13.1 1.5 copy-start.7
  13.1 175.6 %all-gather.11.cloned.1.call-start = ((), (), s32[]{:S(2)}) async-start(), calls=%async_computation.3 | async-start | bytes 8257536 | tf_op jit(solution)/shard_map/all_gather | solution.py:47
Sparse Core Ops, SparseCore 0:
  10.5 37.4 all-gather.6
  50.4 34.3 all-gather.8
  87.3 49.8 all-gather.4
  138.9 49.8 all-gather.10
where the time goes:
time: 203 us; the launch traced here: 202 us
  waiting for transfers between devices  110 us (54%)
  blocking collectives  42.3 us (21%)
  local copies, waits for them, and re-layouts  29.2 us (14%)
  between operations  13.9 us (7%)
  matrix products  7.07 us (3%)
    all_gather x1, waiting for transfers between devices, body(): lax.all_gather(narrow_query, 'zero', axis=0, tiled=True)  46.4 us
    unnamed x1, blocking collectives  42.3 us
    all_gather x1, waiting for transfers between devices, body(): lax.all_gather(narrow_mixed, 'zero', axis=1, tiled=True)  41.6 us
    unnamed x22, local copies, waits for them, and re-layouts  29.2 us
    all_gather x1, waiting for transfers between devices, body(): lax.all_gather(narrow_value, 'zero', axis=0, tiled=True)  21.6 us
  transfers between devices with their start and end apart: 4, of which 3 were waited for; matrix products, arithmetic and copies ran while one was open for 13% of the time, Pallas kernels for 0%

commit v1 on v0

v1 whole, which is shorter than its diff:
```python
import functools
import math

import jax
import jax.numpy as jnp
from jax import lax
from jax.experimental import pallas as pl
from jax.experimental.pallas import tpu as pltpu
from jax.sharding import PartitionSpec as P

mix_rate = 0.5
CORES = 2
LANES = 128
F32 = jnp.float32
BF16 = jnp.bfloat16


def plain_body(
    train_query, low_query, high_query, train_key, low_key, high_key, train_value, low_value, high_value,
    train_mixed, low_mixed, high_mixed, norm_train, norm_step,
):
    def merged(train, low, high):
        return (train.astype(F32) + mix_rate * jnp.dot(low, high, preferred_element_type=F32)).astype(BF16)

    return (
        lax.all_gather(merged(train_query, low_query, high_query), "zero", axis=0, tiled=True).T,
        lax.all_gather(merged(train_key, low_key, high_key), "zero", axis=0, tiled=True).T,
        lax.all_gather(merged(train_value, low_value, high_value), "zero", axis=0, tiled=True).T,
        lax.all_gather(merged(train_mixed, low_mixed, high_mixed).T, "zero", axis=0, tiled=True),
        lax.all_gather((norm_train + norm_step).astype(BF16), ("zero", "width"), axis=0, tiled=True),
    )


def kernel(
    zeros, widths,
    tq, lq, hq, tk, lk, hk, tv, lv, hv, tm, lm, hm, nt, ns,
    oq, ok, ov, om, norm_out,
    on, own_q, own_k, own_v, own_m, pq, pk, pv, plq, plk, plv, keep, swap_send, swap_recv, send, recv, nsend, nrecv,
):
    me, w = lax.axis_index("zero"), lax.axis_index("width")
    c = lax.rem(me, 2)
    x = lax.rem(lax.div(me, 2), 2)
    y = lax.div(me, 4)
    chip = lax.div(me, 2)
    partner, xn, yn = me + 1 - 2 * c, me + 2 - 4 * x, me + 4 - 8 * y
    chip_x, chip_y, chip_d = chip + 1 - 2 * x, chip + 2 - 4 * y, 3 - chip
    rows = tq.shape[0]
    pair = 2 * rows

    def remote(src, dst, ssem, rsem, **where):
        return pltpu.make_async_remote_copy(
            src_ref=src, dst_ref=dst, send_sem=ssem, recv_sem=rsem,
            device_id=where, device_id_type=pl.DeviceIdType.MESH,
        )

    others = [lax.rem(me + d, zeros) for d in range(1, zeros)]
    barrier = pltpu.get_barrier_semaphore()
    for other in others:
        pl.semaphore_signal(barrier, inc=1, device_id={"zero": other}, device_id_type=pl.DeviceIdType.MESH)
    for d in range(1, widths):
        pl.semaphore_signal(
            barrier, inc=1, device_id={"width": lax.rem(w + d, widths)}, device_id_type=pl.DeviceIdType.MESH
        )
    pl.semaphore_wait(barrier, zeros + widths - 2)

    mine = pl.ds(pl.multiple_of(rows * c, 16), rows)
    swaps = []
    for k, (train, low, held, held_low) in enumerate(((tq, lq, pq, plq), (tk, lk, pk, plk), (tv, lv, pv, plv))):
        half = train.shape[1] // 2
        cols = pl.ds(pl.multiple_of((1 - c) * half, LANES), half)
        for e, (src, dst) in enumerate(((train.at[:, cols], held.at[mine, :]), (low, held_low.at[mine, :]))):
            copy = remote(src, dst, swap_send.at[2 * k + e], swap_recv.at[2 * k + e], zero=partner)
            copy.start()
            swaps.append(copy)

    on[me, w] = jnp.pad(nt[...] + ns[...], ((0, 0), (0, LANES - nt.shape[1])))
    for train, low, held, held_low in ((tq, lq, pq, plq), (tk, lk, pk, plk), (tv, lv, pv, plv)):
        half = train.shape[1] // 2
        held[mine, :] = train[:, pl.ds(pl.multiple_of(c * half, LANES), half)]
        held_low[mine, :] = low[...]
    small = []
    for d in range(1, widths):
        copy = remote(
            on.at[me, w], on.at[me, w], nsend.at[d - 1], nrecv.at[d - 1], width=lax.rem(w + d, widths)
        )
        copy.start()
        small.append(copy)

    for i in range(tm.shape[0] // LANES):
        at = slice(i * LANES, (i + 1) * LANES)
        merged = tm[at, :].astype(F32) + mix_rate * jnp.dot(lm[at, :], hm[...], preferred_element_type=F32)
        own_m[:, at] = merged.T.astype(BF16)
    kept = [pltpu.make_async_copy(own_m, om.at[pl.ds(pl.multiple_of(rows * me, 16), rows), :], keep.at[3])]
    kept[0].start()

    for copy in small:
        copy.wait()
    for d in range(1, zeros):
        copy = remote(
            on.at[me], on.at[me], nsend.at[widths - 2 + d], nrecv.at[widths - 2 + d], zero=others[d - 1]
        )
        copy.start()
        small.append(copy)

    part = rows // 2

    def mixed_item(h):
        return lambda p, cc: om.at[pl.ds(pl.multiple_of(rows * (2 * p + cc) + h * part, 16), part), :]

    def item(out, start, size, share):
        return lambda p, cc: out.at[
            pl.ds(pl.multiple_of(share * cc + start, 16), size), pl.ds(pl.multiple_of(pair * p, LANES), pair)
        ]

    nq, nk = oq.shape[0] // 2, ok.shape[0] // 2
    first = [mixed_item(0), item(oq, 0, nq // 2, nq), item(ok, 0, nk, nk)]
    second = [mixed_item(1), item(oq, nq // 2, nq // 2, nq), item(ov, 0, nk, nk)]
    items = first + second
    sources = [
        own_m.at[:part, :], own_q.at[: nq // 2, :], own_k, own_m.at[part:, :], own_q.at[nq // 2 :, :], own_v
    ]
    n = len(first)
    TO_X, TO_Y, ON, P_OWN, P_X, P_Y, P_D = range(7)
    copies = {}

    def go(k, kind, p, where):
        region = items[k](p, c)
        source = sources[k] if kind in (TO_X, TO_Y, P_OWN) else region
        copy = remote(source, region, send.at[k, kind], recv.at[k, kind], zero=where)
        copy.start()
        copies[k, kind] = copy

    def own(j):
        go(j, TO_X, chip, xn)
        go(n + j, TO_Y, chip, yn)

    own(0)

    def merge(e, out, own_out, held, held_low, high):
        half = held.shape[1]
        cols = pl.ds(pl.multiple_of(c * half, LANES), half)
        for j in range(pair // LANES):
            at = slice(j * LANES, (j + 1) * LANES)
            merged = held[at, :].astype(F32) + mix_rate * jnp.dot(
                held_low[at, :], high[:, cols], preferred_element_type=F32
            )
            own_out[:, at] = merged.T.astype(BF16)
        here = out.at[
            pl.ds(pl.multiple_of(c * half, 16), half), pl.ds(pl.multiple_of(pair * chip, LANES), pair)
        ]
        kept.append(pltpu.make_async_copy(own_out, here, keep.at[e]))
        kept[-1].start()

    for copy in swaps:
        copy.wait()
    merge(0, oq, own_q, pq, plq, hq)
    own(1)
    merge(1, ok, own_k, pk, plk, hk)
    merge(2, ov, own_v, pv, plv, hv)
    own(2)
    for j in range(n):
        go(n + j, TO_X, chip, xn)
        go(j, TO_Y, chip, yn)
    for k in range(2 * n):
        go(k, P_OWN, chip, partner)

    for j in range(n):
        copies[j, TO_X].wait_recv()
        go(j, ON, chip_x, yn)
        go(j, P_X, chip_x, partner)
        copies[n + j, TO_Y].wait_recv()
        go(n + j, ON, chip_y, xn)
        go(n + j, P_Y, chip_y, partner)
    for j in range(n):
        copies[n + j, TO_X].wait_recv()
        go(n + j, P_X, chip_x, partner)
        copies[j, TO_Y].wait_recv()
        go(j, P_Y, chip_y, partner)
    for j in range(n):
        for k in (j, n + j):
            copies[k, ON].wait_recv()
            go(k, P_D, chip_d, partner)
    for copy in kept:
        copy.wait()
    for copy in small[widths - 1 :]:
        copy.wait()
    norm_out[...] = on[...]
    for (k, kind), copy in copies.items():
        copy.wait_send()
        if kind >= P_OWN:
            copy.wait_recv()


def fast_body(zeros, widths, *args):
    tq, lq, hq, tk, lk, hk, tv, lv, hv, tm, lm, hm, nt, ns = args
    depth = tq.shape[0] * zeros
    VM = pltpu.VMEM
    new = jax.ShapeDtypeStruct
    outs = [
        new((tq.shape[1], depth), BF16), new((tk.shape[1], depth), BF16), new((tv.shape[1], depth), BF16),
        new((depth, tm.shape[0]), BF16), new((zeros, widths, 1, LANES), F32),
    ]
    pair = 2 * tq.shape[0]
    dma = pltpu.SemaphoreType.DMA
    small = widths - 1 + zeros - 1
    oq, ok, ov, om, on = pl.pallas_call(
        functools.partial(kernel, zeros, widths),
        out_shape=outs,
        in_specs=[pl.BlockSpec(memory_space=VM)] * len(args),
        out_specs=[pl.BlockSpec(memory_space=m) for m in (pl.ANY,) * 4 + (VM,)],
        scratch_shapes=[
            VM((zeros, widths, 1, LANES), F32),
            VM((tq.shape[1] // 2, pair), BF16), VM((tk.shape[1] // 2, pair), BF16), VM((tv.shape[1] // 2, pair), BF16),
            VM((tm.shape[1], tm.shape[0]), BF16),
            VM((pair, tq.shape[1] // 2), BF16), VM((pair, tk.shape[1] // 2), BF16), VM((pair, tv.shape[1] // 2), BF16),
            VM((pair, lq.shape[1]), BF16), VM((pair, lk.shape[1]), BF16), VM((pair, lv.shape[1]), BF16),
            dma((4,)), dma((6,)), dma((6,)), dma((6, 7)), dma((6, 7)), dma((small,)), dma((small,)),
        ],
        compiler_params=pltpu.CompilerParams(
            collective_id=0, has_side_effects=True, vmem_limit_bytes=30 * 2**20
        ),
        name="gather_merged",
    )(tq, lq, hq, tk, lk, hk, tv, lv, hv, tm, lm, hm, nt[None, :], ns[None, :])
    norm = on[:, :, 0, : nt.shape[0]].reshape(-1).astype(BF16)
    return oq, ok, ov, om, norm


def solution(mesh):
    placed = (
        P("zero", "width"), P("zero", None), P(None, "width"),
        P("zero", "width"), P("zero", None), P(None, "width"),
        P("zero", "width"), P("zero", None), P(None, "width"),
        P("width", "zero"), P("width", None), P(None, "zero"),
        P(("zero", "width")), P(("zero", "width")),
    )
    zeros, widths = mesh.shape["zero"], mesh.shape["width"]
    side = math.isqrt(zeros // CORES)

    def body(*args):
        rows = args[0].shape[0]
        square = side == 2 and CORES * side * side == zeros
        if square and CORES * rows % LANES == 0 and rows % 32 == 0:
            return fast_body(zeros, widths, *args)
        return plain_body(*args)

    return jax.shard_map(
        body,
        mesh=mesh,
        in_specs=placed,
        out_specs=(P("width", None), P("width", None), P("width", None), P(None, "width"), P()),
        check_vma=False,
    )
```

time: 203 us -> 140 us (0.69)
  waiting for transfers between devices: 110 us -> 0 us
  Pallas kernels: 0 us -> 102 us
  blocking collectives: 42.3 us -> 0 us
  between operations: 13.9 us -> 0.69 us
  local copies, waits for them, and re-layouts: 29.2 us -> 36.4 us
  matrix products: 7.07 us -> 0 us
    all_gather x4 -> x0, waiting for transfers between devices: 110 us -> none  [the longest x1 46.4 us: body(): lax.all_gather(narrow_query, 'zero', axis=0, tiled=True)]
    pallas_call x0 -> x1, Pallas kernels: none -> 102 us  [fast_body(): pl.pallas_call(functools.partial(kernel, zeros, widths), out_shape=outs,...]
    unnamed x1 -> x0, blocking collectives: 42.3 us -> none
    dot_general x4 -> x0, matrix products: 7.07 us -> none  [the longest x1 2.21 us: body(): jnp.dot(low_key, high_key, preferred_element_type=jnp.float32)]
    unnamed x22 -> x39, local copies, waits for them, and re-layouts: 29.2 us -> 35.7 us
  transfers between devices with their start and end apart: 4 -> 0, of which waited for: 3 -> 0; matrix products, arithmetic and copies ran while one was open for 13% -> 0% of each run, Pallas kernels for 0% -> 0%
where the time goes in v1:
time: 140 us; the launch traced here: 139 us
  Pallas kernels  102 us (73%)
  local copies, waits for them, and re-layouts  36.4 us (26%)
    pallas_call x1, Pallas kernels, fast_body(): pl.pallas_call(functools.partial(kernel, zeros, widths), out_shape=outs,...  102 us
    unnamed x39, local copies, waits for them, and re-layouts  35.7 us

profile of v1, /device:TPU:0, one launch (start us, length us, event | category | flops | bytes accessed | tf_op | source)
XLA Modules:
  0.0 138.7 jit_solution(1007800397932507812)
XLA Ops:
  0.6 0.9 copy.24.lq
  1.5 0.9 copy.25.lk
  2.4 0.9 copy.26.lv
  3.3 1.0 copy.28.lm
  4.3 1.5 %copy.27.tm = bf16[1024,448]{1,0:T(8,128)(2,1)S(1)} copy(bf16[1024,448]{0,1:T(8,128)(2,1)} %param.23) | data formatting | bytes 1835008 | tf_op args[9]
  5.8 0.0 copy-start.5
  5.8 1.2 copy-done.5
  7.0 0.0 copy-start.6
  7.0 1.0 copy-done.6
  8.0 0.0 copy-start.7
  8.0 1.0 copy-done.7
  9.0 0.0 copy-start.8
  9.0 0.8 copy-done.8
  9.9 0.0 copy-start.9
  9.9 0.8 copy-done.9
  10.6 0.0 copy-start.10
  10.6 0.8 copy-done.10
  11.4 0.0 copy-start.11
  11.4 0.8 copy-done.11
  12.2 0.0 copy-start.12
  12.2 0.7 copy-done.12
  12.8 0.0 copy-start.13
  12.8 0.7 copy-done.13
  13.5 101.7 %gather_merged.1 = (bf16[1024,3584]{1,0:T(8,128)(2,1)S(1)}, bf16[512,3584]{1,0:T(8,128)(2,1)S(1)}, bf16[512,3584]{1,0:T(8,128)(2,1)S(1)}, bf16[3584,1024]{1,0:T(8,128)(2,1)}, f32[8,4,1,128]{3,2,1,0:T(1,128)S(1)}) custom-call(bf16[448,1024]{1,0:T(8,128)(2,1)S(1)} %copy-done.5, bf16[448,32]{1,0:T(8,128)(2,1)S(1)} %copy.24.lq, bf16[32,1024]{1,0:T(8,128)(2,1)S(1)} %copy-done.8, ...), custom_call_target="tpu_custom_call" | custom-call | tf_op jit(solution)/shard_map/gather_merged/pallas_call | solution.py:206
  115.1 0.0 copy-start
  115.1 3.0 %copy-done = bf16[1024,3584]{1,0:T(8,128)(2,1)} copy-done((bf16[1024,3584]{1,0:T(8,128)(2,1)}, bf16[1024,3584]{1,0:T(8,128)(2,1)S(1)}, u32[]{:S(2)}) %copy-start) | copy-done | bytes 7340056
  118.2 0.0 copy-start.1
  118.2 1.9 %copy-done.1 = bf16[512,3584]{1,0:T(8,128)(2,1)} copy-done((bf16[512,3584]{1,0:T(8,128)(2,1)}, bf16[512,3584]{1,0:T(8,128)(2,1)S(1)}, u32[]{:S(2)}) %copy-start.1) | copy-done | bytes 3670040
  120.1 0.0 copy-start.3
  120.1 1.8 %copy-done.3 = bf16[512,3584]{1,0:T(8,128)(2,1)} copy-done((bf16[512,3584]{1,0:T(8,128)(2,1)}, bf16[512,3584]{1,0:T(8,128)(2,1)S(1)}, u32[]{:S(2)}) %copy-start.3) | copy-done | bytes 3670040
  121.9 0.1 fusion
  122.0 0.7 convert_element_type.4
  122.7 0.0 copy-start.4
  122.7 0.0 copy-start.2
  122.7 6.8 %copy.33 = bf16[1024,3584]{1,0:T(8,128)(2,1)} copy(bf16[1024,3584]{1,0:T(8,128)(2,1)} %copy-done) | data formatting | bytes 14680064
  129.4 0.0 copy-done.4
  129.4 1.8 %copy.34 = bf16[512,3584]{1,0:T(8,128)(2,1)} copy(bf16[512,3584]{1,0:T(8,128)(2,1)S(1)} %copy-done.4) | data formatting | bytes 7340032
  131.3 0.0 copy-done.2
  131.3 0.0 copy-start.14
  131.3 1.9 %copy.35 = bf16[512,3584]{1,0:T(8,128)(2,1)} copy(bf16[512,3584]{1,0:T(8,128)(2,1)S(1)} %copy-done.2) | data formatting | bytes 7340032
  133.2 2.5 %copy-done.14 = bf16[3584,1024]{1,0:T(8,128)(2,1)S(1)} copy-done((bf16[3584,1024]{1,0:T(8,128)(2,1)S(1)}, bf16[3584,1024]{1,0:T(8,128)(2,1)}, u32[]{:S(2)}) %copy-start.14) | copy-done | bytes 7340056
  135.7 3.0 %copy.36 = bf16[3584,1024]{1,0:T(8,128)(2,1)} copy(bf16[3584,1024]{1,0:T(8,128)(2,1)S(1)} %copy-done.14) | data formatting | bytes 14680064
Async XLA Ops:
  5.8 1.2 copy-start.5
  7.0 1.0 copy-start.6
  8.0 1.0 copy-start.7
  9.0 0.8 copy-start.8
  9.9 0.8 copy-start.9
  10.6 0.8 copy-start.10
  11.4 0.8 copy-start.11
  12.2 0.7 copy-start.12
  12.8 0.7 copy-start.13
  115.1 3.1 %copy-start = (bf16[1024,3584]{1,0:T(8,128)(2,1)}, bf16[1024,3584]{1,0:T(8,128)(2,1)S(1)}, u32[]{:S(2)}) copy-start(bf16[1024,3584]{1,0:T(8,128)(2,1)S(1)} %get-tuple-element.20) | copy-start | bytes 22020100
  118.2 1.9 %copy-start.1 = (bf16[512,3584]{1,0:T(8,128)(2,1)}, bf16[512,3584]{1,0:T(8,128)(2,1)S(1)}, u32[]{:S(2)}) copy-start(bf16[512,3584]{1,0:T(8,128)(2,1)S(1)} %get-tuple-element.22) | copy-start | bytes 11010052
  120.1 1.8 %copy-start.3 = (bf16[512,3584]{1,0:T(8,128)(2,1)}, bf16[512,3584]{1,0:T(8,128)(2,1)S(1)}, u32[]{:S(2)}) copy-start(bf16[512,3584]{1,0:T(8,128)(2,1)S(1)} %get-tuple-element.21) | copy-start | bytes 11010052
  122.7 6.8 %copy-start.4 = (bf16[512,3584]{1,0:T(8,128)(2,1)S(1)}, bf16[512,3584]{1,0:T(8,128)(2,1)}, u32[]{:S(2)}) copy-start(bf16[512,3584]{1,0:T(8,128)(2,1)} %copy-done.3) | copy-start | bytes 11010052
  122.7 8.6 %copy-start.2 = (bf16[512,3584]{1,0:T(8,128)(2,1)S(1)}, bf16[512,3584]{1,0:T(8,128)(2,1)}, u32[]{:S(2)}) copy-start(bf16[512,3584]{1,0:T(8,128)(2,1)} %copy-done.1) | copy-start | bytes 11010052
  131.3 4.4 %copy-start.14 = (bf16[3584,1024]{1,0:T(8,128)(2,1)S(1)}, bf16[3584,1024]{1,0:T(8,128)(2,1)}, u32[]{:S(2)}) copy-start(bf16[3584,1024]{1,0:T(8,128)(2,1)} %get-tuple-element.23) | copy-start | bytes 22020100

commit v2 on v1

--- a/solution.py
+++ b/solution.py
@@ -13,6 +13,10 @@
 LANES = 128
 F32 = jnp.float32
 BF16 = jnp.bfloat16
+SPLIT = 4
+VMEM_BYTES = 67_043_328
+PLACE = pltpu.VMEM
+GATHERED = pltpu.VMEM
 
 
 def plain_body(
@@ -33,9 +37,9 @@
 
 def kernel(
     zeros, widths,
-    tq, lq, hq, tk, lk, hk, tv, lv, hv, tm, lm, hm, nt, ns,
+    tq_h, lq_h, hq_h, tk_h, lk_h, hk_h, tv_h, lv_h, hv_h, tm_h, lm_h, hm_h, nt_h, ns_h,
     oq, ok, ov, om, norm_out,
-    on, own_q, own_k, own_v, own_m, pq, pk, pv, plq, plk, plv, keep, swap_send, swap_recv, send, recv, nsend, nrecv,
+    lq, hq, lk, hk, lv, hv, tm, lm, hm, nt, ns, fetched, on, own_q, own_k, own_v, own_m, pq, pk, pv, plq, plk, plv, keep, swap_send, swap_recv, send, recv, nsend, nrecv,
 ):
     me, w = lax.axis_index("zero"), lax.axis_index("width")
     c = lax.rem(me, 2)
@@ -44,14 +48,31 @@
     chip = lax.div(me, 2)
     partner, xn, yn = me + 1 - 2 * c, me + 2 - 4 * x, me + 4 - 8 * y
     chip_x, chip_y, chip_d = chip + 1 - 2 * x, chip + 2 - 4 * y, 3 - chip
-    rows = tq.shape[0]
+    rows = tq_h.shape[0]
     pair = 2 * rows
+
+    def rank_dot(left, right):
+        return lax.dot_general(left, right, (((0,), (0,)), ((), ())), preferred_element_type=F32)
 
     def remote(src, dst, ssem, rsem, **where):
         return pltpu.make_async_remote_copy(
             src_ref=src, dst_ref=dst, send_sem=ssem, recv_sem=rsem,
             device_id=where, device_id_type=pl.DeviceIdType.MESH,
         )
+
+    fetches = []
+    for k, (src, dst) in enumerate((
+        (nt_h, nt), (ns_h, ns), (lm_h, lm), (hm_h, hm), (tm_h, tm), (tq_h, pq), (lq_h, lq.at[c]), (hq_h, hq),
+        (tk_h, pk), (lk_h, lk.at[c]), (hk_h, hk), (tv_h, pv), (lv_h, lv.at[c]), (hv_h, hv),
+    )):
+        if k in (5, 8, 11):
+            half = src.shape[1] // 2
+            cols = pl.ds(pl.multiple_of(c * half, LANES), half)
+            dst = dst.at[pl.ds(pl.multiple_of(rows * c, 16), rows), :]
+            src = src.at[:, cols]
+        copy = pltpu.make_async_copy(src, dst, fetched.at[k])
+        copy.start()
+        fetches.append(copy)
 
     others = [lax.rem(me + d, zeros) for d in range(1, zeros)]
     barrier = pltpu.get_barrier_semaphore()
@@ -65,19 +86,17 @@
 
     mine = pl.ds(pl.multiple_of(rows * c, 16), rows)
     swaps = []
-    for k, (train, low, held, held_low) in enumerate(((tq, lq, pq, plq), (tk, lk, pk, plk), (tv, lv, pv, plv))):
+    for k, (train, low, held, held_low) in enumerate(((tq_h, lq_h, pq, lq), (tk_h, lk_h, pk, lk), (tv_h, lv_h, pv, lv))):
         half = train.shape[1] // 2
         cols = pl.ds(pl.multiple_of((1 - c) * half, LANES), half)
-        for e, (src, dst) in enumerate(((train.at[:, cols], held.at[mine, :]), (low, held_low.at[mine, :]))):
+        for e, (src, dst) in enumerate(((train.at[:, cols], held.at[mine, :]), (low, held_low.at[c]))):
             copy = remote(src, dst, swap_send.at[2 * k + e], swap_recv.at[2 * k + e], zero=partner)
             copy.start()
             swaps.append(copy)
 
+    for copy in fetches[:2]:
+        copy.wait()
     on[me, w] = jnp.pad(nt[...] + ns[...], ((0, 0), (0, LANES - nt.shape[1])))
-    for train, low, held, held_low in ((tq, lq, pq, plq), (tk, lk, pk, plk), (tv, lv, pv, plv)):
-        half = train.shape[1] // 2
-        held[mine, :] = train[:, pl.ds(pl.multiple_of(c * half, LANES), half)]
-        held_low[mine, :] = low[...]
     small = []
     for d in range(1, widths):
         copy = remote(
@@ -86,10 +105,13 @@
         copy.start()
         small.append(copy)
 
-    for i in range(tm.shape[0] // LANES):
-        at = slice(i * LANES, (i + 1) * LANES)
-        merged = tm[at, :].astype(F32) + mix_rate * jnp.dot(lm[at, :], hm[...], preferred_element_type=F32)
-        own_m[:, at] = merged.T.astype(BF16)
+    for copy in fetches[2:5]:
+        copy.wait()
+    step = 2 * LANES
+    for i in range(tm.shape[1] // step):
+        at = slice(i * step, (i + 1) * step)
+        merged = tm[:, at].astype(F32) + mix_rate * rank_dot(hm[...], lm[:, at])
+        own_m[:, at] = merged.astype(BF16)
     kept = [pltpu.make_async_copy(own_m, om.at[pl.ds(pl.multiple_of(rows * me, 16), rows), :], keep.at[3])]
     kept[0].start()
 
@@ -136,14 +158,14 @@
 
     own(0)
 
-    def merge(e, out, own_out, held, held_low, high):
+    def merge(e, out, own_out, held, low, held_low, high):
         half = held.shape[1]
+        held_low[:, :rows] = low[0]
+        held_low[:, rows:] = low[1]
         cols = pl.ds(pl.multiple_of(c * half, LANES), half)
         for j in range(pair // LANES):
             at = slice(j * LANES, (j + 1) * LANES)
-            merged = held[at, :].astype(F32) + mix_rate * jnp.dot(
-                held_low[at, :], high[:, cols], preferred_element_type=F32
-            )
+            merged = held[at, :].astype(F32) + mix_rate * rank_dot(held_low[:, at], high[:, cols])
             own_out[:, at] = merged.T.astype(BF16)
         here = out.at[
             pl.ds(pl.multiple_of(c * half, 16), half), pl.ds(pl.multiple_of(pair * chip, LANES), pair)
@@ -151,12 +173,12 @@
         kept.append(pltpu.make_async_copy(own_out, here, keep.at[e]))
         kept[-1].start()
 
-    for copy in swaps:
-        copy.wait()
-    merge(0, oq, own_q, pq, plq, hq)
+    for copy in fetches[5:] + swaps:
+        copy.wait()
+    merge(0, oq, own_q, pq, lq, plq, hq)
     own(1)
-    merge(1, ok, own_k, pk, plk, hk)
-    merge(2, ov, own_v, pv, plv, hv)
+    merge(1, ok, own_k, pk, lk, plk, hk)
+    merge(2, ov, own_v, pv, lv, plv, hv)
     own(2)
     for j in range(n):
         go(n + j, TO_X, chip, xn)
@@ -191,38 +213,61 @@
             copy.wait_recv()
 
 
+def publish(*refs):
+    n = len(refs) // 2
+    done = refs[-1]
+    copies = []
+    for k, (src, dst) in enumerate(zip(refs[:n], refs[n : 2 * n])):
+        size = src.shape[0] // SPLIT
+        for e in range(SPLIT):
+            at = pl.ds(e * size, size)
+            copies.append(pltpu.make_async_copy(src.at[at, :], dst.at[at, :], done.at[k, e]))
+            copies[-1].start()
+    for copy in copies:
+        copy.wait()
+
+
 def fast_body(zeros, widths, *args):
     tq, lq, hq, tk, lk, hk, tv, lv, hv, tm, lm, hm, nt, ns = args
-    depth = tq.shape[0] * zeros
-    VM = pltpu.VMEM
+    rows, depth = tq.shape[0], tq.shape[0] * zeros
+    VM, HBM = pltpu.VMEM, pltpu.MemorySpace.HBM
     new = jax.ShapeDtypeStruct
-    outs = [
-        new((tq.shape[1], depth), BF16), new((tk.shape[1], depth), BF16), new((tv.shape[1], depth), BF16),
-        new((depth, tm.shape[0]), BF16), new((zeros, widths, 1, LANES), F32),
-    ]
-    pair = 2 * tq.shape[0]
+    shapes = [(tq.shape[1], depth), (tk.shape[1], depth), (tv.shape[1], depth), (depth, tm.shape[0])]
+    pair = 2 * rows
+    held = 2 * sum(a * b for a, b in shapes)
     dma = pltpu.SemaphoreType.DMA
     small = widths - 1 + zeros - 1
-    oq, ok, ov, om, on = pl.pallas_call(
+    moved = [tq, lq.T, hq, tk, lk.T, hk, tv, lv.T, hv, tm.T, lm.T, hm, nt[None, :], ns[None, :]]
+    local = [VM(((2,) if i in (1, 4, 7) else ()) + a.shape, a.dtype) for i, a in enumerate(moved) if i not in (0, 3, 6)]
+    *full, on = pl.pallas_call(
         functools.partial(kernel, zeros, widths),
-        out_shape=outs,
-        in_specs=[pl.BlockSpec(memory_space=VM)] * len(args),
-        out_specs=[pl.BlockSpec(memory_space=m) for m in (pl.ANY,) * 4 + (VM,)],
-        scratch_shapes=[
-            VM((zeros, widths, 1, LANES), F32),
+        out_shape=[GATHERED(s, BF16) for s in shapes] + [new((zeros, widths, 1, LANES), F32)],
+        in_specs=[pl.BlockSpec(memory_space=HBM)] * len(args),
+        out_specs=[pl.BlockSpec(memory_space=PLACE)] * len(shapes) + [pl.BlockSpec(memory_space=VM)],
+        scratch_shapes=local + [
+            dma((len(args),)), VM((zeros, widths, 1, LANES), F32),
             VM((tq.shape[1] // 2, pair), BF16), VM((tk.shape[1] // 2, pair), BF16), VM((tv.shape[1] // 2, pair), BF16),
             VM((tm.shape[1], tm.shape[0]), BF16),
             VM((pair, tq.shape[1] // 2), BF16), VM((pair, tk.shape[1] // 2), BF16), VM((pair, tv.shape[1] // 2), BF16),
-            VM((pair, lq.shape[1]), BF16), VM((pair, lk.shape[1]), BF16), VM((pair, lv.shape[1]), BF16),
+            VM((lq.shape[1], pair), BF16), VM((lk.shape[1], pair), BF16), VM((lv.shape[1], pair), BF16),
             dma((4,)), dma((6,)), dma((6,)), dma((6, 7)), dma((6, 7)), dma((small,)), dma((small,)),
         ],
         compiler_params=pltpu.CompilerParams(
-            collective_id=0, has_side_effects=True, vmem_limit_bytes=30 * 2**20
+            collective_id=0, has_side_effects=True, vmem_limit_bytes=VMEM_BYTES - held - 48 * 1024
         ),
         name="gather_merged",
-    )(tq, lq, hq, tk, lk, hk, tv, lv, hv, tm, lm, hm, nt[None, :], ns[None, :])
+    )(*moved)
     norm = on[:, :, 0, : nt.shape[0]].reshape(-1).astype(BF16)
-    return oq, ok, ov, om, norm
+    full = pl.pallas_call(
+        publish,
+        out_shape=[new(s, BF16) for s in shapes],
+        in_specs=[pl.BlockSpec(memory_space=PLACE)] * len(shapes),
+        out_specs=[pl.BlockSpec(memory_space=HBM)] * len(shapes),
+        scratch_shapes=[dma((len(shapes), SPLIT))],
+        compiler_params=pltpu.CompilerParams(vmem_limit_bytes=2**20),
+        name="publish",
+    )(*full)
+    return (*full, norm)
 
 
 def solution(mesh):

time: 140 us -> 112 us (0.80)
  local copies, waits for them, and re-layouts: 36.4 us -> 0.75 us
  Pallas kernels: 102 us -> 110 us
    unnamed x39 -> x2, local copies, waits for them, and re-layouts: 35.7 us -> 0.01 us
    pallas_call x1 -> x2, Pallas kernels: 102 us -> 110 us  [the longest x1 102 us: fast_body(): pl.pallas_call(functools.partial(kernel, zeros, widths), out_shape=[GATHE...]
where the time goes in v2:
time: 112 us; the launch traced here: 111 us
  Pallas kernels  110 us (98%)
    pallas_call x1, Pallas kernels, fast_body(): pl.pallas_call(functools.partial(kernel, zeros, widths), out_shape=[GATHE...  102 us
    pallas_call x1, Pallas kernels, fast_body(): pl.pallas_call(publish, out_shape=[new(s, BF16) for s in shapes], in_spec...  7.6 us

profile of v2, /device:TPU:0, one launch (start us, length us, event | category | flops | bytes accessed | tf_op | source)
XLA Modules:
  0.0 111.4 jit_solution(8705750238904270357)
XLA Ops:
  0.6 102.4 %gather_merged.1 = (bf16[1024,3584]{1,0:T(8,128)(2,1)S(1)}, bf16[512,3584]{1,0:T(8,128)(2,1)S(1)}, bf16[512,3584]{1,0:T(8,128)(2,1)S(1)}, bf16[3584,1024]{1,0:T(8,128)(2,1)S(1)}, f32[8,4,1,128]{3,2,1,0:T(1,128)}) custom-call(bf16[448,1024]{1,0:T(8,128)(2,1)} %tq_h.1, bf16[32,448]{1,0:T(8,128)(2,1)} %bitcast.9, bf16[32,1024]{1,0:T(8,128)(2,1)} %hq_h.1, ...), custom_call_target="tpu_custom_call" | custom-call | tf_op jit(solution)/shard_map/gather_merged/pallas_call | solution.py:242
  103.0 0.0 copy-start
  103.1 7.6 %publish.1 = (bf16[1024,3584]{1,0:T(8,128)(2,1)}, bf16[512,3584]{1,0:T(8,128)(2,1)}, bf16[512,3584]{1,0:T(8,128)(2,1)}, bf16[3584,1024]{1,0:T(8,128)(2,1)}) custom-call(bf16[1024,3584]{1,0:T(8,128)(2,1)S(1)} %get-tuple-element.14.refs_0_, bf16[512,3584]{1,0:T(8,128)(2,1)S(1)} %get-tuple-element.15.refs_1_, bf16[512,3584]{1,0:T(8,128)(2,1)S(1)} %get-tuple-element.16.refs_2_, ...), custom_call_target="tpu_custom_call" | custom-call | tf_op jit(solution)/shard_map/publish/pallas_call | solution.py:261
  110.7 0.0 copy-done
  110.7 0.1 fusion
  110.7 0.7 convert_element_type.4
Async XLA Ops:
  103.0 7.6 %copy-start = (f32[8,4,1,128]{3,2,1,0:T(1,128)S(1)}, f32[8,4,1,128]{3,2,1,0:T(1,128)}, u32[]{:S(2)}) copy-start(f32[8,4,1,128]{3,2,1,0:T(1,128)} %get-tuple-element.22) | copy-start | bytes 49156

commit v3 on v2

--- a/solution.py
+++ b/solution.py
@@ -82,7 +82,53 @@
         pl.semaphore_signal(
             barrier, inc=1, device_id={"width": lax.rem(w + d, widths)}, device_id_type=pl.DeviceIdType.MESH
         )
+
+    for copy in fetches[2:5]:
+        copy.wait()
+    step = 2 * LANES
+    for i in range(tm.shape[1] // step):
+        at = slice(i * step, (i + 1) * step)
+        merged = tm[:, at].astype(F32) + mix_rate * rank_dot(hm[...], lm[:, at])
+        own_m[:, at] = merged.astype(BF16)
     pl.semaphore_wait(barrier, zeros + widths - 2)
+    kept = [pltpu.make_async_copy(own_m, om.at[pl.ds(pl.multiple_of(rows * me, 16), rows), :], keep.at[3])]
+    kept[0].start()
+
+    part = rows // 2
+
+    def mixed_item(h):
+        return lambda p, cc: om.at[pl.ds(pl.multiple_of(rows * (2 * p + cc) + h * part, 16), part), :]
+
+    def item(out, start, size, share):
+        return lambda p, cc: out.at[
+            pl.ds(pl.multiple_of(share * cc + start, 16), size), pl.ds(pl.multiple_of(pair * p, LANES), pair)
+        ]
+
+    nq, nk = oq.shape[0] // 2, ok.shape[0] // 2
+    last = nk // 4
+    first = [mixed_item(0), item(oq, 0, nq // 2, nq), item(ok, 0, nk - last, nk), item(ok, nk - last, last, nk)]
+    second = [mixed_item(1), item(oq, nq // 2, nq // 2, nq), item(ov, 0, nk - last, nk), item(ov, nk - last, last, nk)]
+    items = first + second
+    sources = [
+        own_m.at[:part, :], own_q.at[: nq // 2, :], own_k.at[: nk - last, :], own_k.at[nk - last :, :],
+        own_m.at[part:, :], own_q.at[nq // 2 :, :], own_v.at[: nk - last, :], own_v.at[nk - last :, :],
+    ]
+    n = len(first)
+    TO_X, TO_Y, ON, P_OWN, P_X, P_Y, P_D = range(7)
+    copies = {}
+
+    def go(k, kind, p, where):
+        region = items[k](p, c)
+        source = sources[k] if kind in (TO_X, TO_Y, P_OWN) else region
+        copy = remote(source, region, send.at[k, kind], recv.at[k, kind], zero=where)
+        copy.start()
+        copies[k, kind] = copy
+
+    def own(j):
+        go(j, TO_X, chip, xn)
+        go(n + j, TO_Y, chip, yn)
+
+    own(0)
 
     mine = pl.ds(pl.multiple_of(rows * c, 16), rows)
     swaps = []
@@ -104,59 +150,6 @@
         )
         copy.start()
         small.append(copy)
-
-    for copy in fetches[2:5]:
-        copy.wait()
-    step = 2 * LANES
-    for i in range(tm.shape[1] // step):
-        at = slice(i * step, (i + 1) * step)
-        merged = tm[:, at].astype(F32) + mix_rate * rank_dot(hm[...], lm[:, at])
-        own_m[:, at] = merged.astype(BF16)
-    kept = [pltpu.make_async_copy(own_m, om.at[pl.ds(pl.multiple_of(rows * me, 16), rows), :], keep.at[3])]
-    kept[0].start()
-
-    for copy in small:
-        copy.wait()
-    for d in range(1, zeros):
-        copy = remote(
-            on.at[me], on.at[me], nsend.at[widths - 2 + d], nrecv.at[widths - 2 + d], zero=others[d - 1]
-        )
-        copy.start()
-        small.append(copy)
-
-    part = rows // 2
-
-    def mixed_item(h):
-        return lambda p, cc: om.at[pl.ds(pl.multiple_of(rows * (2 * p + cc) + h * part, 16), part), :]
-
-    def item(out, start, size, share):
-        return lambda p, cc: out.at[
-            pl.ds(pl.multiple_of(share * cc + start, 16), size), pl.ds(pl.multiple_of(pair * p, LANES), pair)
-        ]
-
-    nq, nk = oq.shape[0] // 2, ok.shape[0] // 2
-    first = [mixed_item(0), item(oq, 0, nq // 2, nq), item(ok, 0, nk, nk)]
-    second = [mixed_item(1), item(oq, nq // 2, nq // 2, nq), item(ov, 0, nk, nk)]
-    items = first + second
-    sources = [
-        own_m.at[:part, :], own_q.at[: nq // 2, :], own_k, own_m.at[part:, :], own_q.at[nq // 2 :, :], own_v
-    ]
-    n = len(first)
-    TO_X, TO_Y, ON, P_OWN, P_X, P_Y, P_D = range(7)
-    copies = {}
-
-    def go(k, kind, p, where):
-        region = items[k](p, c)
-        source = sources[k] if kind in (TO_X, TO_Y, P_OWN) else region
-        copy = remote(source, region, send.at[k, kind], recv.at[k, kind], zero=where)
-        copy.start()
-        copies[k, kind] = copy
-
-    def own(j):
-        go(j, TO_X, chip, xn)
-        go(n + j, TO_Y, chip, yn)
-
-    own(0)
 
     def merge(e, out, own_out, held, low, held_low, high):
         half = held.shape[1]
@@ -177,9 +170,18 @@
         copy.wait()
     merge(0, oq, own_q, pq, lq, plq, hq)
     own(1)
+    for copy in small:
+        copy.wait()
+    for d in range(1, zeros):
+        copy = remote(
+            on.at[me], on.at[me], nsend.at[widths - 2 + d], nrecv.at[widths - 2 + d], zero=others[d - 1]
+        )
+        copy.start()
+        small.append(copy)
     merge(1, ok, own_k, pk, lk, plk, hk)
     merge(2, ov, own_v, pv, lv, plv, hv)
     own(2)
+    own(3)
     for j in range(n):
         go(n + j, TO_X, chip, xn)
         go(j, TO_Y, chip, yn)
@@ -250,7 +252,7 @@
             VM((tm.shape[1], tm.shape[0]), BF16),
             VM((pair, tq.shape[1] // 2), BF16), VM((pair, tk.shape[1] // 2), BF16), VM((pair, tv.shape[1] // 2), BF16),
             VM((lq.shape[1], pair), BF16), VM((lk.shape[1], pair), BF16), VM((lv.shape[1], pair), BF16),
-            dma((4,)), dma((6,)), dma((6,)), dma((6, 7)), dma((6, 7)), dma((small,)), dma((small,)),
+            dma((4,)), dma((6,)), dma((6,)), dma((8, 7)), dma((8, 7)), dma((small,)), dma((small,)),
         ],
         compiler_params=pltpu.CompilerParams(
             collective_id=0, has_side_effects=True, vmem_limit_bytes=VMEM_BYTES - held - 48 * 1024

time: 112 us -> 108 us (0.964)
  Pallas kernels: 110 us -> 107 us
    pallas_call x1, Pallas kernels: 102 us -> 99.2 us  [fast_body(): pl.pallas_call(functools.partial(kernel, zeros, widths), out_shape=[GATHE...]
where the time goes in v3:
time: 108 us
  Pallas kernels  107 us (99%)
    pallas_call x1, Pallas kernels, fast_body(): pl.pallas_call(functools.partial(kernel, zeros, widths), out_shape=[GATHE...  99.2 us
    pallas_call x1, Pallas kernels, fast_body(): pl.pallas_call(publish, out_shape=[new(s, BF16) for s in shapes], in_spec...  7.6 us

profile of v3, /device:TPU:0, one launch (start us, length us, event | category | flops | bytes accessed | tf_op | source)
XLA Modules:
  0.0 108.2 jit_solution(11547409781236263284)
XLA Ops:
  0.6 99.2 %gather_merged.1 = (bf16[1024,3584]{1,0:T(8,128)(2,1)S(1)}, bf16[512,3584]{1,0:T(8,128)(2,1)S(1)}, bf16[512,3584]{1,0:T(8,128)(2,1)S(1)}, bf16[3584,1024]{1,0:T(8,128)(2,1)S(1)}, f32[8,4,1,128]{3,2,1,0:T(1,128)}) custom-call(bf16[448,1024]{1,0:T(8,128)(2,1)} %tq_h.1, bf16[32,448]{1,0:T(8,128)(2,1)} %bitcast.9, bf16[32,1024]{1,0:T(8,128)(2,1)} %hq_h.1, ...), custom_call_target="tpu_custom_call" | custom-call | tf_op jit(solution)/shard_map/gather_merged/pallas_call | solution.py:244
  99.9 0.0 copy-start
  99.9 7.6 %publish.1 = (bf16[1024,3584]{1,0:T(8,128)(2,1)}, bf16[512,3584]{1,0:T(8,128)(2,1)}, bf16[512,3584]{1,0:T(8,128)(2,1)}, bf16[3584,1024]{1,0:T(8,128)(2,1)}) custom-call(bf16[1024,3584]{1,0:T(8,128)(2,1)S(1)} %get-tuple-element.14.refs_0_, bf16[512,3584]{1,0:T(8,128)(2,1)S(1)} %get-tuple-element.15.refs_1_, bf16[512,3584]{1,0:T(8,128)(2,1)S(1)} %get-tuple-element.16.refs_2_, ...), custom_call_target="tpu_custom_call" | custom-call | tf_op jit(solution)/shard_map/publish/pallas_call | solution.py:263
  107.5 0.0 copy-done
  107.5 0.1 fusion
  107.5 0.7 convert_element_type.4
Async XLA Ops:
  99.9 7.6 %copy-start = (f32[8,4,1,128]{3,2,1,0:T(1,128)S(1)}, f32[8,4,1,128]{3,2,1,0:T(1,128)}, u32[]{:S(2)}) copy-start(f32[8,4,1,128]{3,2,1,0:T(1,128)} %get-tuple-element.22) | copy-start | bytes 49156
